TPU v7x, 32 devices: a whole 2x2x4 slice. The times are simulated.
32 devices in a mesh: grp: 8 (over y, x, core), mem: 4 (over z).
Axes of the slice: x: 2, y: 2, z: 4, core: 2. Of those that a mesh axis runs over, the one named last changes fastest.
Arguments:
- residual: float32 [256, 64, 256], P(('grp', 'mem')), may hold values from -6 to 6
- direction: float32 [256, 64, 256], P(('grp', 'mem')), may hold values from -6 to 6
- local_inverse: bfloat16 [256, 256, 256], P(('grp', 'mem')), may hold values from -1 to 16, as said below
- dirichlet: bfloat16 [256, 256, 256], P(('grp', 'mem')), may hold values from -1 to 16, as said below
- coupling: bfloat16 [256, 24, 256], P(('grp', 'mem')), may hold values from -0.375 to 0.375
- corner_map: int32 [256, 24], P(('grp', 'mem')), may hold values from 0 to 6143
- coarse_factor: bfloat16 [8, 2048, 2048], P('grp'), may hold values from -1 to 3, as said below
Outputs:
- new_residual: float32 [256, 64, 256], P(('grp', 'mem'))
- new_direction: float32 [256, 64, 256], P(('grp', 'mem'))
- step_sizes: float32 [3, 64], replicated
Inputs may be any that keep to these rules, and one draw needn't show every extreme that they name: `local_inverse`: each subdomain's matrix is symmetric positive definite. `dirichlet`: each subdomain's matrix is symmetric positive definite. `coarse_factor`: each group's factor is lower triangular with a positive diagonal.
All inputs are finite; a program needn't handle non-finite values.
Results may differ from a plain program's by a relative error of at most 0.0083.
Values sent between devices are 32-bit elements; how exact they have to be, the bound alone decides.
A program may use at most 128 MiB of HBM per device.

v0:
```python
import jax
import jax.numpy as jnp
from jax import lax
from jax.sharding import PartitionSpec as P

ITERS = 3
highest = lax.Precision.HIGHEST


def from_behind(block, axis, distance):
    devices = range(lax.axis_size(axis))
    route = [((i - distance) % len(devices), i) for i in devices]
    return lax.ppermute(block, axis, route)


def extended(cells, sides, width):
    for axis, dim in sides:
        count = lax.axis_size(axis)
        head = lax.slice_in_dim(cells, 0, width, axis=dim)
        tail = lax.slice_in_dim(cells, cells.shape[dim] - width, cells.shape[dim], axis=dim)
        cells = jnp.concatenate(
            [
                lax.ppermute(tail, axis, [(i, (i + 1) % count) for i in range(count)]),
                cells,
                lax.ppermute(head, axis, [((i + 1) % count, i) for i in range(count)]),
            ],
            axis=dim,
        )
    return cells


def solve_local(matrices, vectors):
    return jnp.einsum(
        "sij,skj->ski", matrices, vectors.astype(jnp.bfloat16), preferred_element_type=jnp.float32
    )


def column_sums(left_side, right_side):
    return jnp.sum(left_side * right_side, axis=(0, 2))


def coarse_solve(factor, coarse_load):
    forward = jax.scipy.linalg.solve_triangular(factor, coarse_load.T, lower=True)
    return jax.scipy.linalg.solve_triangular(factor, forward, lower=True, trans=1).T


def fold_neighbours(partial_value, block_size):
    from_upper = from_behind(partial_value[:, :block_size], "grp", -1)
    from_lower = from_behind(partial_value[:, 2 * block_size :], "grp", 1)
    return partial_value[:, block_size : 2 * block_size] + from_upper + from_lower


def local(residual, direction, local_inverse, dirichlet, coupling, corner_map, coarse_factor):
    sub_count, rhs_count, dofs_count = residual.shape
    corner_count = coupling.shape[1]
    block_size = coarse_factor.shape[1]
    factor = coarse_factor[0].astype(jnp.float32)
    flat_map = corner_map.reshape(-1)
    coupling_wide = coupling.astype(jnp.float32)
    precond = solve_local(dirichlet, residual)
    norm_now = lax.psum(column_sums(residual, precond), ("grp", "mem"))
    step_list = []
    for iteration in range(ITERS):
        solved = solve_local(local_inverse, direction)
        partial_corner = jnp.einsum("ski,sci->skc", solved, coupling_wide, precision=highest)
        flat_corner = partial_corner.transpose(1, 0, 2).reshape(rhs_count, sub_count * corner_count)
        partial_value = (
            jnp.zeros((rhs_count, 3 * block_size), jnp.float32).at[:, flat_map].add(flat_corner)
        )
        folded = fold_neighbours(partial_value, block_size)
        solution = coarse_solve(factor, lax.psum(folded, "mem"))
        widened = extended(solution, (("grp", 1),), block_size)
        picked = widened[:, flat_map].reshape(rhs_count, sub_count, corner_count).transpose(1, 0, 2)
        lifted = jnp.einsum("skc,sci->ski", picked, coupling_wide, precision=highest)
        image = solve_local(local_inverse, direction + lifted)
        curvature = lax.psum(column_sums(direction, image), ("grp", "mem"))
        alpha = norm_now / curvature
        step_list.append(alpha)
        residual = residual - alpha[None, :, None] * image
        precond = solve_local(dirichlet, residual)
        norm_next = lax.psum(column_sums(residual, precond), ("grp", "mem"))
        direction = precond + (norm_next / norm_now)[None, :, None] * direction
        norm_now = norm_next
    return (residual, direction, jnp.stack(step_list))


def solution(mesh):
    return jax.shard_map(
        local,
        mesh=mesh,
        in_specs=(
            P(("grp", "mem"), None, None),
            P(("grp", "mem"), None, None),
            P(("grp", "mem"), None, None),
            P(("grp", "mem"), None, None),
            P(("grp", "mem"), None, None),
            P(("grp", "mem"), None),
            P("grp", None, None),
        ),
        out_specs=(P(("grp", "mem"), None, None), P(("grp", "mem"), None, None), P()),
        check_vma=False,
    )
```

profile of v0, /device:TPU:0, one launch (start us, length us, event | category | flops | bytes accessed | tf_op | source)
XLA Modules:
  0.0 917.9 jit_solution(7679273841835778049)
XLA Ops:
  11.1 3.0 scatter_custom_fusion
  14.1 3.0 fusion.365
  24.0 11.3 %convert_select_fusion = f32[2048,2048]{1,0:T(8,128)} fusion(bf16[1,2048,2048]{2,1,0:T(8,128)(2,1)} %param.17), kind=kLoop, calls=%fused_computation.8 | loop fusion | flops 12582912 | bytes 25165824 | tf_op jit(solution)/shard_map/jit(_solve_triangular)/triangular_solve | solution.py:44
  37.6 55.7 %while.12 = (s32[]{:T(128)}, f32[2048,2048]{1,0:T(8,128)}, s32[16,2]{0,1:T(2,128)S(1)}, f32[16,128,128]{2,1,0:T(8,128)}, s32[]{:T(128)}) while((s32[]{:T(128)}, f32[2048,2048]{1,0:T(8,128)}, s32[16,2]{0,1:T(2,128)S(1)}, f32[16,128,128]{2,1,0:T(8,128)}, s32[]{:T(128)}) %tuple.417), condition=%wide.while_cond.1, body=%wide.while_body.1.sunk | while | flops 2 | bytes 132205 | solution.py:44
  38.2 2.9 bitcast_dynamic-update-slice_fusion.2
  45.2 2.9 bitcast_dynamic-update-slice_fusion.2
  55.7 2.9 bitcast_dynamic-update-slice_fusion.2
  59.2 2.9 bitcast_dynamic-update-slice_fusion.2
  62.6 2.9 bitcast_dynamic-update-slice_fusion.2
  73.1 2.9 bitcast_dynamic-update-slice_fusion.2
  83.6 2.9 bitcast_dynamic-update-slice_fusion.2
  93.3 158.4 %custom-call.11 = f32[16,128,128]{1,2,0:T(8,128)S(1)} custom-call(f32[16,128,128]{2,1,0:T(8,128)} %get-tuple-element.46), custom_call_target="InvertDiagBlocksLowerTriangular" | custom-call | tf_op jit(solution)/shard_map/jit(_solve_triangular)/triangular_solve | solution.py:44
  308.3 11.7 %collective-permute-done.3 = f32[64,2048]{1,0:T(8,128)S(1)} collective-permute-done((f32[64,2048]{1,0:T(8,128)S(1)}, f32[64,2048]{1,0:T(8,128)S(1)}, u32[]{:S(2)}, u32[]{:S(2)}) %collective-permute-start.3) | collective-permute-done | bytes 524320 | tf_op jit(solution)/shard_map/ppermute | solution.py:25
  322.5 3.2 copy.31
  332.1 39.5 %all-reduce = (f32[64]{0:T(128)S(1)}, f32[64]{0:T(128)S(1)}) all-reduce(f32[64]{0:T(128)S(1)} %fusion.9, f32[64]{0:T(128)S(1)} %get-tuple-element.437), channel_id=1, replica_groups=mesh['grp'=8,'mem'=4] {'grp','mem'}, use_global_device_ids=true, to_apply=%region_1.0 | all-reduce | flops 128 | bytes 1024 | tf_op jit(solution)/shard_map/psum | solution.py:61
  375.1 40.9 %psum.73 = f32[64]{0:T(128)S(1)} all-reduce(f32[64]{0:T(128)S(1)} %get-tuple-element.439), channel_id=1, replica_groups=mesh['grp'=8,'mem'=4] {'grp','mem'}, use_global_device_ids=true, to_apply=%region_7.0 | all-reduce | flops 64 | bytes 512 | tf_op jit(solution)/shard_map/psum | solution.py:81
  419.0 3.0 scatter_custom_fusion.1
  422.0 3.6 fusion.364
  435.3 8.7 collective-permute-done.5
  447.3 38.6 %all-reduce.7.cloned.1.call-done = f32[2048,64]{0,1:T(8,128)} async-done(((f32[2048,64]{0,1:T(8,128)}), f32[2048,64]{0,1:T(8,128)}) %all-reduce.7.cloned.1.call-update) | async-done | bytes 524304 | tf_op jit(solution)/shard_map/psum | solution.py:71
  556.5 12.2 %collective-permute-done.7 = f32[64,2048]{1,0:T(8,128)S(1)} collective-permute-done((f32[64,2048]{1,0:T(8,128)S(1)}, f32[64,2048]{1,0:T(8,128)S(1)}, u32[]{:S(2)}, u32[]{:S(2)}) %collective-permute-start.7) | collective-permute-done | bytes 524320 | tf_op jit(solution)/shard_map/ppermute | solution.py:25
  572.0 3.2 copy.35
  581.7 39.3 %psum.75 = f32[64]{0:T(128)S(1)} all-reduce(f32[64]{0:T(128)S(1)} %get-tuple-element.479), channel_id=1, replica_groups=mesh['grp'=8,'mem'=4] {'grp','mem'}, use_global_device_ids=true, to_apply=%region_11.0 | all-reduce | flops 64 | bytes 512 | tf_op jit(solution)/shard_map/psum | solution.py:76
  624.5 38.9 %psum.76 = f32[64]{0:T(128)S(1)} all-reduce(f32[64]{0:T(128)S(1)} %get-tuple-element.481), channel_id=1, replica_groups=mesh['grp'=8,'mem'=4] {'grp','mem'}, use_global_device_ids=true, to_apply=%region_13.0 | all-reduce | flops 64 | bytes 512 | tf_op jit(solution)/shard_map/psum | solution.py:81
  666.4 3.0 scatter_custom_fusion.2
  669.4 3.6 fusion.363
  682.9 7.5 collective-permute-done.9
  694.3 39.1 %all-reduce.9.cloned.1.call-done = f32[2048,64]{0,1:T(8,128)} async-done(((f32[2048,64]{0,1:T(8,128)}), f32[2048,64]{0,1:T(8,128)}) %all-reduce.9.cloned.1.call-update) | async-done | bytes 524304 | tf_op jit(solution)/shard_map/psum | solution.py:71
  804.0 12.3 %collective-permute-done.11 = f32[64,2048]{1,0:T(8,128)S(1)} collective-permute-done((f32[64,2048]{1,0:T(8,128)S(1)}, f32[64,2048]{1,0:T(8,128)S(1)}, u32[]{:S(2)}, u32[]{:S(2)}) %collective-permute-start.11) | collective-permute-done | bytes 524320 | tf_op jit(solution)/shard_map/ppermute | solution.py:25
  819.5 3.2 copy.39
  828.4 39.3 %psum.78 = f32[64]{0:T(128)S(1)} all-reduce(f32[64]{0:T(128)S(1)} %get-tuple-element.521), channel_id=1, replica_groups=mesh['grp'=8,'mem'=4] {'grp','mem'}, use_global_device_ids=true, to_apply=%region_17.0 | all-reduce | flops 64 | bytes 512 | tf_op jit(solution)/shard_map/psum | solution.py:76
  869.4 38.9 %psum.79 = f32[64]{0:T(128)S(1)} all-reduce(f32[64]{0:T(128)S(1)} %get-tuple-element.523), channel_id=1, replica_groups=mesh['grp'=8,'mem'=4] {'grp','mem'}, use_global_device_ids=true, to_apply=%region_19.0 | all-reduce | flops 64 | bytes 512 | tf_op jit(solution)/shard_map/psum | solution.py:81
  (668 shorter events, 313.8 us)
Async XLA Ops:
  7.2 1.2 copy-start
  7.2 244.6 %all-reduce.5.cloned.1.call-start = ((), (), s32[]{:S(2)}) async-start(), calls=%async_computation | async-start | bytes 1048576 | tf_op jit(solution)/shard_map/psum | solution.py:71
  19.5 16.1 %collective-permute-start.1 = (f32[64,2048]{1,0:T(8,128)}, f32[64,2048]{1,0:T(8,128)}, u32[]{:S(2)}, u32[]{:S(2)}) collective-permute-start(f32[64,2048]{1,0:T(8,128)} %copy.30), channel_id=1, source_target_pairs={{28,0},{0,4},{4,8},{8,12},{12,16},{16,20},{20,24},{24,28},{29,1},{... | collective-permute-start | bytes 1572872 | tf_op jit(solution)/shard_map/ppermute | solution.py:13
  21.1 14.5 %collective-permute-start = (f32[64,2048]{1,0:T(8,128)}, f32[64,2048]{1,0:T(8,128)S(1)}, u32[]{:S(2)}, u32[]{:S(2)}) collective-permute-start(f32[64,2048]{1,0:T(8,128)} %copy.29), channel_id=1, source_target_pairs={{4,0},{8,4},{12,8},{16,12},{20,16},{24,20},{28,24},{0,28},{5,1},{9... | collective-permute-start | bytes 1572872 | tf_op jit(solution)/shard_map/ppermute | solution.py:13
  37.6 448.3 %all-reduce.7.cloned.1.call-start = ((), (), s32[]{:S(2)}) async-start(), calls=%async_computation.1 | async-start | bytes 1048576 | tf_op jit(solution)/shard_map/psum | solution.py:71
  251.8 39.4 %copy-start.1 = (f32[2048,2048]{1,0:T(8,128)S(1)}, f32[2048,2048]{1,0:T(8,128)}, u32[]{:S(2)}) copy-start(f32[2048,2048]{1,0:T(8,128)} %get-tuple-element.572) | copy-start | bytes 50331652
  272.1 35.6 %copy-start.2 = (bf16[8,256,256]{2,1,0:T(8,128)(2,1)S(1)}, bf16[8,256,256]{2,1,0:T(8,128)(2,1)}, u32[]{:S(2)}) copy-start(bf16[8,256,256]{2,1,0:T(8,128)(2,1)} %param.14) | copy-start | bytes 3145732
  272.1 35.6 %copy-start.9 = (f32[8,64,256]{2,1,0:T(8,128)S(1)}, f32[8,64,256]{2,1,0:T(8,128)}, u32[]{:S(2)}) copy-start(f32[8,64,256]{2,1,0:T(8,128)} %param.11) | copy-start | bytes 1572868
  292.3 35.9 %copy-start.7 = (bf16[8,24,256]{2,1,0:T(8,128)(2,1)S(1)}, bf16[8,24,256]{2,1,0:T(8,128)(2,1)}, u32[]{:S(2)}) copy-start(bf16[8,24,256]{2,1,0:T(8,128)(2,1)} %param.15) | copy-start | bytes 294916
  306.0 13.9 %collective-permute-start.3 = (f32[64,2048]{1,0:T(8,128)S(1)}, f32[64,2048]{1,0:T(8,128)S(1)}, u32[]{:S(2)}, u32[]{:S(2)}) collective-permute-start(f32[64,2048]{1,0:T(8,128)S(1)} %bitcast.583), channel_id=1, source_target_pairs={{4,0},{8,4},{12,8},{16,12},{20,16},{24,20},{28,24},{0,28},{5,1},{9... | collective-permute-start | bytes 1572872 | tf_op jit(solution)/shard_map/ppermute | solution.py:25
  307.7 13.5 %collective-permute-start.2 = (f32[64,2048]{1,0:T(8,128)S(1)}, f32[64,2048]{1,0:T(8,128)S(1)}, u32[]{:S(2)}, u32[]{:S(2)}) collective-permute-start(f32[64,2048]{1,0:T(8,128)S(1)} %bitcast.584), channel_id=1, source_target_pairs={{0,4},{4,8},{8,12},{12,16},{16,20},{20,24},{24,28},{28,0},{1,5},{5... | collective-permute-start | bytes 1572872 | tf_op jit(solution)/shard_map/ppermute | solution.py:23
  373.0 0.8 copy-start.6
  417.4 0.8 copy-start.4
  430.3 13.7 %collective-permute-start.5 = (f32[64,2048]{1,0:T(8,128)}, f32[64,2048]{1,0:T(8,128)}, u32[]{:S(2)}, u32[]{:S(2)}) collective-permute-start(f32[64,2048]{1,0:T(8,128)} %copy.34), channel_id=1, source_target_pairs={{28,0},{0,4},{4,8},{8,12},{12,16},{16,20},{20,24},{24,28},{29,1},{... | collective-permute-start | bytes 1572872 | tf_op jit(solution)/shard_map/ppermute | solution.py:13
  430.3 14.3 %collective-permute-start.4 = (f32[64,2048]{1,0:T(8,128)}, f32[64,2048]{1,0:T(8,128)}, u32[]{:S(2)}, u32[]{:S(2)}) collective-permute-start(f32[64,2048]{1,0:T(8,128)} %copy.33), channel_id=1, source_target_pairs={{4,0},{8,4},{12,8},{16,12},{20,16},{24,20},{28,24},{0,28},{5,1},{9... | collective-permute-start | bytes 1572872 | tf_op jit(solution)/shard_map/ppermute | solution.py:13
  446.9 286.5 %all-reduce.9.cloned.1.call-start = ((), (), s32[]{:S(2)}) async-start(), calls=%async_computation.2 | async-start | bytes 1048576 | tf_op jit(solution)/shard_map/psum | solution.py:71
  555.6 13.2 %collective-permute-start.7 = (f32[64,2048]{1,0:T(8,128)S(1)}, f32[64,2048]{1,0:T(8,128)S(1)}, u32[]{:S(2)}, u32[]{:S(2)}) collective-permute-start(f32[64,2048]{1,0:T(8,128)S(1)} %bitcast.586), channel_id=1, source_target_pairs={{4,0},{8,4},{12,8},{16,12},{20,16},{24,20},{28,24},{0,28},{5,1},{9... | collective-permute-start | bytes 1572872 | tf_op jit(solution)/shard_map/ppermute | solution.py:25
  556.5 14.3 %collective-permute-start.6 = (f32[64,2048]{1,0:T(8,128)S(1)}, f32[64,2048]{1,0:T(8,128)S(1)}, u32[]{:S(2)}, u32[]{:S(2)}) collective-permute-start(f32[64,2048]{1,0:T(8,128)S(1)} %bitcast.587), channel_id=1, source_target_pairs={{0,4},{4,8},{8,12},{12,16},{16,20},{20,24},{24,28},{28,0},{1,5},{5... | collective-permute-start | bytes 1572872 | tf_op jit(solution)/shard_map/ppermute | solution.py:23
  622.4 0.8 copy-start.5
  664.8 0.8 copy-start.3
  677.7 12.7 %collective-permute-start.9 = (f32[64,2048]{1,0:T(8,128)}, f32[64,2048]{1,0:T(8,128)}, u32[]{:S(2)}, u32[]{:S(2)}) collective-permute-start(f32[64,2048]{1,0:T(8,128)} %copy.38), channel_id=1, source_target_pairs={{28,0},{0,4},{4,8},{8,12},{12,16},{16,20},{20,24},{24,28},{29,1},{... | collective-permute-start | bytes 1572872 | tf_op jit(solution)/shard_map/ppermute | solution.py:13
  677.7 14.3 %collective-permute-start.8 = (f32[64,2048]{1,0:T(8,128)}, f32[64,2048]{1,0:T(8,128)}, u32[]{:S(2)}, u32[]{:S(2)}) collective-permute-start(f32[64,2048]{1,0:T(8,128)} %copy.37), channel_id=1, source_target_pairs={{4,0},{8,4},{12,8},{16,12},{20,16},{24,20},{28,24},{0,28},{5,1},{9... | collective-permute-start | bytes 1572872 | tf_op jit(solution)/shard_map/ppermute | solution.py:13
  803.1 13.2 %collective-permute-start.11 = (f32[64,2048]{1,0:T(8,128)S(1)}, f32[64,2048]{1,0:T(8,128)S(1)}, u32[]{:S(2)}, u32[]{:S(2)}) collective-permute-start(f32[64,2048]{1,0:T(8,128)S(1)} %bitcast.580), channel_id=1, source_target_pairs={{4,0},{8,4},{12,8},{16,12},{20,16},{24,20},{28,24},{0,28},{5,1},{9... | collective-permute-start | bytes 1572872 | tf_op jit(solution)/shard_map/ppermute | solution.py:25
  804.0 14.3 %collective-permute-start.10 = (f32[64,2048]{1,0:T(8,128)S(1)}, f32[64,2048]{1,0:T(8,128)S(1)}, u32[]{:S(2)}, u32[]{:S(2)}) collective-permute-start(f32[64,2048]{1,0:T(8,128)S(1)} %bitcast.581), channel_id=1, source_target_pairs={{0,4},{4,8},{8,12},{12,16},{16,20},{20,24},{24,28},{28,0},{1,5},{5... | collective-permute-start | bytes 1572872 | tf_op jit(solution)/shard_map/ppermute | solution.py:23
  868.9 42.0 %copy-start.8 = (f32[8,64,256]{2,1,0:T(8,128)}, f32[8,64,256]{2,1,0:T(8,128)S(1)}, u32[]{:S(2)}) copy-start(f32[8,64,256]{2,1,0:T(8,128)S(1)} %multiply_subtract_fusion) | copy-start | bytes 1572868
Sparse Core Ops, SparseCore 0:
  37.7 39.7 all-reduce.4
  447.0 38.8 all-reduce.6
  694.4 38.9 all-reduce.8
where the time goes:
time: 931 us; the launch traced here: 918 us
  blocking collectives  237 us (25%)
  matrix products  207 us (22%)
  other arithmetic  198 us (21%)
  waiting for transfers between devices  138 us (15%)
  local copies, waits for them, and re-layouts  107 us (11%)
  between operations  18.2 us (2%)
  starting transfers between devices  12.9 us (1%)
    another operation x4, other arithmetic, coarse_solve(): jax.scipy.linalg.solve_triangular(factor, forward, lower=True, trans=1)  170 us
    another operation x93, matrix products, coarse_solve(): jax.scipy.linalg.solve_triangular(factor, coarse_load.T, lower=True)  124 us
    psum x3, blocking collectives, local(): norm_next = lax.psum(column_sums(residual, precond), ('grp', 'mem'))  119 us
    psum x2, blocking collectives, local(): curvature = lax.psum(column_sums(direction, image), ('grp', 'mem'))  78.5 us
    psum x3, waiting for transfers between devices, local(): solution = coarse_solve(factor, lax.psum(folded, 'mem'))  77.7 us
    another operation x93, matrix products, coarse_solve(): jax.scipy.linalg.solve_triangular(factor, forward, lower=True, trans=1)  64.3 us
    another operation x85, local copies, waits for them, and re-layouts, coarse_solve(): jax.scipy.linalg.solve_triangular(factor, forward, lower=True, trans=1)  55.9 us
    psum x1, blocking collectives, local(): norm_now = lax.psum(column_sums(residual, precond), ('grp', 'mem'))  39.5 us
  transfers between devices with their start and end apart: 15, of which 12 were waited for; matrix products, arithmetic and copies ran while one was open for 25% of the time, Pallas kernels for 0%

commit v1 on v0

--- a/solution.py
+++ b/solution.py
@@ -78,7 +78,7 @@
         step_list.append(alpha)
         residual = residual - alpha[None, :, None] * image
         precond = solve_local(dirichlet, residual)
-        norm_next = lax.psum(column_sums(residual, precond), ("grp", "mem"))
+        norm_next = lax.psum(lax.psum(column_sums(residual, precond), "mem"), "grp")
         direction = precond + (norm_next / norm_now)[None, :, None] * direction
         norm_now = norm_next
     return (residual, direction, jnp.stack(step_list))

time: 931 us -> 877 us (0.942)
  blocking collectives: 237 us -> 185 us
    psum x3 -> x6, blocking collectives: 119 us -> 66.4 us  [local(): norm_next = lax.psum(lax.psum(column_sums(residual, precond), 'mem'), 'grp')]
  transfers between devices with their start and end apart: 15 -> 15, of which waited for: 12 -> 10; matrix products, arithmetic and copies ran while one was open for 25% -> 27% of each run, Pallas kernels for 0% -> 0%
where the time goes in v1:
time: 877 us; the launch traced here: 864 us
  matrix products  207 us (24%)
  other arithmetic  198 us (23%)
  blocking collectives  185 us (21%)
  waiting for transfers between devices  134 us (15%)
  local copies, waits for them, and re-layouts  110 us (13%)
  between operations  18 us (2%)
  starting transfers between devices  12.7 us (1%)
    another operation x4, other arithmetic, coarse_solve(): jax.scipy.linalg.solve_triangular(factor, forward, lower=True, trans=1)  170 us
    another operation x93, matrix products, coarse_solve(): jax.scipy.linalg.solve_triangular(factor, coarse_load.T, lower=True)  124 us
    psum x2, blocking collectives, local(): curvature = lax.psum(column_sums(direction, image), ('grp', 'mem'))  78.5 us
    psum x3, waiting for transfers between devices, local(): solution = coarse_solve(factor, lax.psum(folded, 'mem'))  73.5 us
    psum x6, blocking collectives, local(): norm_next = lax.psum(lax.psum(column_sums(residual, precond), 'mem'), 'grp')  66.4 us
    another operation x93, matrix products, coarse_solve(): jax.scipy.linalg.solve_triangular(factor, forward, lower=True, trans=1)  64.4 us
    another operation x85, local copies, waits for them, and re-layouts, coarse_solve(): jax.scipy.linalg.solve_triangular(factor, forward, lower=True, trans=1)  58.1 us
    psum x1, blocking collectives, local(): norm_now = lax.psum(column_sums(residual, precond), ('grp', 'mem'))  39.5 us
  transfers between devices with their start and end apart: 15, of which 10 were waited for; matrix products, arithmetic and copies ran while one was open for 27% of the time, Pallas kernels for 0%

profile of v1, /device:TPU:0, one launch (start us, length us, event | category | flops | bytes accessed | tf_op | source)
XLA Modules:
  0.0 863.7 jit_solution(17691947418626368432)
XLA Ops:
  11.1 3.0 scatter_custom_fusion
  14.2 3.0 fusion.365
  24.0 11.3 %convert_select_fusion = f32[2048,2048]{1,0:T(8,128)} fusion(bf16[1,2048,2048]{2,1,0:T(8,128)(2,1)} %param.17), kind=kLoop, calls=%fused_computation.8 | loop fusion | flops 12582912 | bytes 25165824 | tf_op jit(solution)/shard_map/jit(_solve_triangular)/triangular_solve | solution.py:44
  37.6 58.0 %while.12 = (s32[]{:T(128)}, f32[2048,2048]{1,0:T(8,128)}, s32[16,2]{0,1:T(2,128)S(1)}, f32[16,128,128]{2,1,0:T(8,128)}, s32[]{:T(128)}) while((s32[]{:T(128)}, f32[2048,2048]{1,0:T(8,128)}, s32[16,2]{0,1:T(2,128)S(1)}, f32[16,128,128]{2,1,0:T(8,128)}, s32[]{:T(128)}) %tuple.417), condition=%wide.while_cond.1, body=%wide.while_body.1.sunk | while | flops 2 | bytes 132205 | solution.py:44
  41.9 3.0 bitcast_dynamic-update-slice_fusion.2
  56.4 3.0 bitcast_dynamic-update-slice_fusion.2
  63.7 3.0 bitcast_dynamic-update-slice_fusion.2
  89.1 3.0 bitcast_dynamic-update-slice_fusion.2
  95.6 158.4 %custom-call.11 = f32[16,128,128]{1,2,0:T(8,128)S(1)} custom-call(f32[16,128,128]{2,1,0:T(8,128)} %get-tuple-element.46), custom_call_target="InvertDiagBlocksLowerTriangular" | custom-call | tf_op jit(solution)/shard_map/jit(_solve_triangular)/triangular_solve | solution.py:44
  310.6 11.7 %collective-permute-done.3 = f32[64,2048]{1,0:T(8,128)S(1)} collective-permute-done((f32[64,2048]{1,0:T(8,128)S(1)}, f32[64,2048]{1,0:T(8,128)S(1)}, u32[]{:S(2)}, u32[]{:S(2)}) %collective-permute-start.3) | collective-permute-done | bytes 524320 | tf_op jit(solution)/shard_map/ppermute | solution.py:25
  324.7 3.2 copy.31
  334.4 39.5 %all-reduce = (f32[64]{0:T(128)S(1)}, f32[64]{0:T(128)S(1)}) all-reduce(f32[64]{0:T(128)S(1)} %fusion.9, f32[64]{0:T(128)S(1)} %get-tuple-element.437), channel_id=1, replica_groups=mesh['grp'=8,'mem'=4] {'grp','mem'}, use_global_device_ids=true, to_apply=%region_1.0 | all-reduce | flops 128 | bytes 1024 | tf_op jit(solution)/shard_map/psum | solution.py:61
  377.4 10.6 %psum.94 = f32[64]{0:T(128)S(1)} all-reduce(f32[64]{0:T(128)S(1)} %get-tuple-element.439), channel_id=1, replica_groups=mesh['grp'=8,'mem'=4] {'mem'}, use_global_device_ids=true, to_apply=%region_7.0 | all-reduce | flops 64 | bytes 512 | tf_op jit(solution)/shard_map/psum | solution.py:81
  388.0 11.9 %psum.95 = f32[64]{0:T(128)S(1)} all-reduce(f32[64]{0:T(128)S(1)} %psum.94), channel_id=1, replica_groups=mesh['grp'=8,'mem'=4] {'grp'}, use_global_device_ids=true, to_apply=%region_8.0 | all-reduce | flops 64 | bytes 512 | tf_op jit(solution)/shard_map/psum | solution.py:81
  402.8 3.0 scatter_custom_fusion.1
  405.8 3.6 fusion.364
  419.0 9.7 %collective-permute-done.5 = f32[64,2048]{1,0:T(8,128)} collective-permute-done((f32[64,2048]{1,0:T(8,128)}, f32[64,2048]{1,0:T(8,128)}, u32[]{:S(2)}, u32[]{:S(2)}) %collective-permute-start.5) | collective-permute-done | bytes 524320 | tf_op jit(solution)/shard_map/ppermute | solution.py:13
  431.2 36.1 %all-reduce.7.cloned.1.call-done = f32[2048,64]{0,1:T(8,128)} async-done(((f32[2048,64]{0,1:T(8,128)}), f32[2048,64]{0,1:T(8,128)}) %all-reduce.7.cloned.1.call-update) | async-done | bytes 524304 | tf_op jit(solution)/shard_map/psum | solution.py:71
  538.2 12.3 %collective-permute-done.7 = f32[64,2048]{1,0:T(8,128)S(1)} collective-permute-done((f32[64,2048]{1,0:T(8,128)S(1)}, f32[64,2048]{1,0:T(8,128)S(1)}, u32[]{:S(2)}, u32[]{:S(2)}) %collective-permute-start.7) | collective-permute-done | bytes 524320 | tf_op jit(solution)/shard_map/ppermute | solution.py:25
  553.7 3.2 copy.35
  563.4 39.3 %psum.97 = f32[64]{0:T(128)S(1)} all-reduce(f32[64]{0:T(128)S(1)} %get-tuple-element.479), channel_id=1, replica_groups=mesh['grp'=8,'mem'=4] {'grp','mem'}, use_global_device_ids=true, to_apply=%region_12.0 | all-reduce | flops 64 | bytes 512 | tf_op jit(solution)/shard_map/psum | solution.py:76
  606.1 10.2 %psum.98 = f32[64]{0:T(128)S(1)} all-reduce(f32[64]{0:T(128)S(1)} %get-tuple-element.481), channel_id=1, replica_groups=mesh['grp'=8,'mem'=4] {'mem'}, use_global_device_ids=true, to_apply=%region_14.0 | all-reduce | flops 64 | bytes 512 | tf_op jit(solution)/shard_map/psum | solution.py:81
  616.3 11.8 %psum.99 = f32[64]{0:T(128)S(1)} all-reduce(f32[64]{0:T(128)S(1)} %psum.98), channel_id=1, replica_groups=mesh['grp'=8,'mem'=4] {'grp'}, use_global_device_ids=true, to_apply=%region_15.0 | all-reduce | flops 64 | bytes 512 | tf_op jit(solution)/shard_map/psum | solution.py:81
  631.1 3.0 scatter_custom_fusion.2
  634.1 3.6 fusion.363
  647.5 9.3 %collective-permute-done.9 = f32[64,2048]{1,0:T(8,128)} collective-permute-done((f32[64,2048]{1,0:T(8,128)}, f32[64,2048]{1,0:T(8,128)}, u32[]{:S(2)}, u32[]{:S(2)}) %collective-permute-start.9) | collective-permute-done | bytes 524320 | tf_op jit(solution)/shard_map/ppermute | solution.py:13
  659.0 37.4 %all-reduce.9.cloned.1.call-done = f32[2048,64]{0,1:T(8,128)} async-done(((f32[2048,64]{0,1:T(8,128)}), f32[2048,64]{0,1:T(8,128)}) %all-reduce.9.cloned.1.call-update) | async-done | bytes 524304 | tf_op jit(solution)/shard_map/psum | solution.py:71
  767.0 12.2 %collective-permute-done.11 = f32[64,2048]{1,0:T(8,128)S(1)} collective-permute-done((f32[64,2048]{1,0:T(8,128)S(1)}, f32[64,2048]{1,0:T(8,128)S(1)}, u32[]{:S(2)}, u32[]{:S(2)}) %collective-permute-start.11) | collective-permute-done | bytes 524320 | tf_op jit(solution)/shard_map/ppermute | solution.py:25
  782.5 3.2 copy.39
  791.4 39.3 %psum.101 = f32[64]{0:T(128)S(1)} all-reduce(f32[64]{0:T(128)S(1)} %get-tuple-element.521), channel_id=1, replica_groups=mesh['grp'=8,'mem'=4] {'grp','mem'}, use_global_device_ids=true, to_apply=%region_19.0 | all-reduce | flops 64 | bytes 512 | tf_op jit(solution)/shard_map/psum | solution.py:76
  832.4 10.2 %psum.102 = f32[64]{0:T(128)S(1)} all-reduce(f32[64]{0:T(128)S(1)} %get-tuple-element.523), channel_id=1, replica_groups=mesh['grp'=8,'mem'=4] {'mem'}, use_global_device_ids=true, to_apply=%region_21.0 | all-reduce | flops 64 | bytes 512 | tf_op jit(solution)/shard_map/psum | solution.py:81
  842.6 11.8 %psum.103 = f32[64]{0:T(128)S(1)} all-reduce(f32[64]{0:T(128)S(1)} %psum.102), channel_id=1, replica_groups=mesh['grp'=8,'mem'=4] {'grp'}, use_global_device_ids=true, to_apply=%region_22.0 | all-reduce | flops 64 | bytes 512 | tf_op jit(solution)/shard_map/psum | solution.py:81
  (671 shorter events, 321.8 us)
Async XLA Ops:
  7.2 1.2 copy-start
  7.2 246.9 %all-reduce.5.cloned.1.call-start = ((), (), s32[]{:S(2)}) async-start(), calls=%async_computation | async-start | bytes 1048576 | tf_op jit(solution)/shard_map/psum | solution.py:71
  19.5 16.1 %collective-permute-start.1 = (f32[64,2048]{1,0:T(8,128)}, f32[64,2048]{1,0:T(8,128)}, u32[]{:S(2)}, u32[]{:S(2)}) collective-permute-start(f32[64,2048]{1,0:T(8,128)} %copy.30), channel_id=1, source_target_pairs={{28,0},{0,4},{4,8},{8,12},{12,16},{16,20},{20,24},{24,28},{29,1},{... | collective-permute-start | bytes 1572872 | tf_op jit(solution)/shard_map/ppermute | solution.py:13
  21.1 14.5 %collective-permute-start = (f32[64,2048]{1,0:T(8,128)}, f32[64,2048]{1,0:T(8,128)S(1)}, u32[]{:S(2)}, u32[]{:S(2)}) collective-permute-start(f32[64,2048]{1,0:T(8,128)} %copy.29), channel_id=1, source_target_pairs={{4,0},{8,4},{12,8},{16,12},{20,16},{24,20},{28,24},{0,28},{5,1},{9... | collective-permute-start | bytes 1572872 | tf_op jit(solution)/shard_map/ppermute | solution.py:13
  37.6 429.8 %all-reduce.7.cloned.1.call-start = ((), (), s32[]{:S(2)}) async-start(), calls=%async_computation.1 | async-start | bytes 1048576 | tf_op jit(solution)/shard_map/psum | solution.py:71
  254.1 39.4 %copy-start.1 = (f32[2048,2048]{1,0:T(8,128)S(1)}, f32[2048,2048]{1,0:T(8,128)}, u32[]{:S(2)}) copy-start(f32[2048,2048]{1,0:T(8,128)} %get-tuple-element.572) | copy-start | bytes 50331652
  274.3 35.6 %copy-start.2 = (bf16[8,256,256]{2,1,0:T(8,128)(2,1)S(1)}, bf16[8,256,256]{2,1,0:T(8,128)(2,1)}, u32[]{:S(2)}) copy-start(bf16[8,256,256]{2,1,0:T(8,128)(2,1)} %param.14) | copy-start | bytes 3145732
  274.4 35.6 %copy-start.9 = (f32[8,64,256]{2,1,0:T(8,128)S(1)}, f32[8,64,256]{2,1,0:T(8,128)}, u32[]{:S(2)}) copy-start(f32[8,64,256]{2,1,0:T(8,128)} %param.11) | copy-start | bytes 1572868
  294.6 35.9 %copy-start.7 = (bf16[8,24,256]{2,1,0:T(8,128)(2,1)S(1)}, bf16[8,24,256]{2,1,0:T(8,128)(2,1)}, u32[]{:S(2)}) copy-start(bf16[8,24,256]{2,1,0:T(8,128)(2,1)} %param.15) | copy-start | bytes 294916
  308.3 14.0 %collective-permute-start.3 = (f32[64,2048]{1,0:T(8,128)S(1)}, f32[64,2048]{1,0:T(8,128)S(1)}, u32[]{:S(2)}, u32[]{:S(2)}) collective-permute-start(f32[64,2048]{1,0:T(8,128)S(1)} %bitcast.583), channel_id=1, source_target_pairs={{4,0},{8,4},{12,8},{16,12},{20,16},{24,20},{28,24},{0,28},{5,1},{9... | collective-permute-start | bytes 1572872 | tf_op jit(solution)/shard_map/ppermute | solution.py:25
  310.0 13.5 %collective-permute-start.2 = (f32[64,2048]{1,0:T(8,128)S(1)}, f32[64,2048]{1,0:T(8,128)S(1)}, u32[]{:S(2)}, u32[]{:S(2)}) collective-permute-start(f32[64,2048]{1,0:T(8,128)S(1)} %bitcast.584), channel_id=1, source_target_pairs={{0,4},{4,8},{8,12},{12,16},{16,20},{20,24},{24,28},{28,0},{1,5},{5... | collective-permute-start | bytes 1572872 | tf_op jit(solution)/shard_map/ppermute | solution.py:23
  375.3 0.8 copy-start.6
  401.2 0.8 copy-start.4
  414.0 14.7 %collective-permute-start.5 = (f32[64,2048]{1,0:T(8,128)}, f32[64,2048]{1,0:T(8,128)}, u32[]{:S(2)}, u32[]{:S(2)}) collective-permute-start(f32[64,2048]{1,0:T(8,128)} %copy.34), channel_id=1, source_target_pairs={{28,0},{0,4},{4,8},{8,12},{12,16},{16,20},{20,24},{24,28},{29,1},{... | collective-permute-start | bytes 1572872 | tf_op jit(solution)/shard_map/ppermute | solution.py:13
  414.4 14.3 %collective-permute-start.4 = (f32[64,2048]{1,0:T(8,128)}, f32[64,2048]{1,0:T(8,128)}, u32[]{:S(2)}, u32[]{:S(2)}) collective-permute-start(f32[64,2048]{1,0:T(8,128)} %copy.33), channel_id=1, source_target_pairs={{4,0},{8,4},{12,8},{16,12},{20,16},{24,20},{28,24},{0,28},{5,1},{9... | collective-permute-start | bytes 1572872 | tf_op jit(solution)/shard_map/ppermute | solution.py:13
  431.0 265.4 %all-reduce.9.cloned.1.call-start = ((), (), s32[]{:S(2)}) async-start(), calls=%async_computation.2 | async-start | bytes 1048576 | tf_op jit(solution)/shard_map/psum | solution.py:71
  537.2 13.2 %collective-permute-start.7 = (f32[64,2048]{1,0:T(8,128)S(1)}, f32[64,2048]{1,0:T(8,128)S(1)}, u32[]{:S(2)}, u32[]{:S(2)}) collective-permute-start(f32[64,2048]{1,0:T(8,128)S(1)} %bitcast.586), channel_id=1, source_target_pairs={{4,0},{8,4},{12,8},{16,12},{20,16},{24,20},{28,24},{0,28},{5,1},{9... | collective-permute-start | bytes 1572872 | tf_op jit(solution)/shard_map/ppermute | solution.py:25
  538.2 14.2 %collective-permute-start.6 = (f32[64,2048]{1,0:T(8,128)S(1)}, f32[64,2048]{1,0:T(8,128)S(1)}, u32[]{:S(2)}, u32[]{:S(2)}) collective-permute-start(f32[64,2048]{1,0:T(8,128)S(1)} %bitcast.587), channel_id=1, source_target_pairs={{0,4},{4,8},{8,12},{12,16},{16,20},{20,24},{24,28},{28,0},{1,5},{5... | collective-permute-start | bytes 1572872 | tf_op jit(solution)/shard_map/ppermute | solution.py:23
  604.0 0.8 copy-start.5
  629.5 0.8 copy-start.3
  642.3 14.4 %collective-permute-start.9 = (f32[64,2048]{1,0:T(8,128)}, f32[64,2048]{1,0:T(8,128)}, u32[]{:S(2)}, u32[]{:S(2)}) collective-permute-start(f32[64,2048]{1,0:T(8,128)} %copy.38), channel_id=1, source_target_pairs={{28,0},{0,4},{4,8},{8,12},{12,16},{16,20},{20,24},{24,28},{29,1},{... | collective-permute-start | bytes 1572872 | tf_op jit(solution)/shard_map/ppermute | solution.py:13
  642.3 14.4 %collective-permute-start.8 = (f32[64,2048]{1,0:T(8,128)}, f32[64,2048]{1,0:T(8,128)}, u32[]{:S(2)}, u32[]{:S(2)}) collective-permute-start(f32[64,2048]{1,0:T(8,128)} %copy.37), channel_id=1, source_target_pairs={{4,0},{8,4},{12,8},{16,12},{20,16},{24,20},{28,24},{0,28},{5,1},{9... | collective-permute-start | bytes 1572872 | tf_op jit(solution)/shard_map/ppermute | solution.py:13
  766.0 13.2 %collective-permute-start.11 = (f32[64,2048]{1,0:T(8,128)S(1)}, f32[64,2048]{1,0:T(8,128)S(1)}, u32[]{:S(2)}, u32[]{:S(2)}) collective-permute-start(f32[64,2048]{1,0:T(8,128)S(1)} %bitcast.580), channel_id=1, source_target_pairs={{4,0},{8,4},{12,8},{16,12},{20,16},{24,20},{28,24},{0,28},{5,1},{9... | collective-permute-start | bytes 1572872 | tf_op jit(solution)/shard_map/ppermute | solution.py:25
  767.0 14.3 %collective-permute-start.10 = (f32[64,2048]{1,0:T(8,128)S(1)}, f32[64,2048]{1,0:T(8,128)S(1)}, u32[]{:S(2)}, u32[]{:S(2)}) collective-permute-start(f32[64,2048]{1,0:T(8,128)S(1)} %bitcast.581), channel_id=1, source_target_pairs={{0,4},{4,8},{8,12},{12,16},{16,20},{20,24},{24,28},{28,0},{1,5},{5... | collective-permute-start | bytes 1572872 | tf_op jit(solution)/shard_map/ppermute | solution.py:23
  831.8 25.1 %copy-start.8 = (f32[8,64,256]{2,1,0:T(8,128)}, f32[8,64,256]{2,1,0:T(8,128)S(1)}, u32[]{:S(2)}) copy-start(f32[8,64,256]{2,1,0:T(8,128)S(1)} %multiply_subtract_fusion) | copy-start | bytes 1572868
Sparse Core Ops, SparseCore 0:
  37.7 39.6 all-reduce.4
  431.1 36.2 all-reduce.6
  659.1 37.2 all-reduce.8
